TPU v7x, 32 devices: a whole 2x2x4 slice. The times are simulated.
32 devices in a mesh: seq: 8 (over z, x), grp: 4 (over y, core).
Axes of the slice: x: 2, y: 2, z: 4, core: 2. Of those that a mesh axis runs over, the one named last changes fastest.
Arguments:
- delta_codes: int32 [16, 16, 2048, 128], P('grp', None, 'seq'), may hold values from -63 to 63, as said below
- scale_index: int32 [16, 16, 128], P('grp', None, 'seq'), may hold values from 0 to 15
- anchor_codes: int32 [16, 16, 128], P('grp'), may hold values from -8 to 7
- scale_table: float32 [16, 128], replicated, may hold values from 5e-05 to 0.0005
- anchor_scale: float32 [128], replicated, may hold values from 0.0001 to 0.001
Outputs:
- decode_cache: bfloat16 [4, 64, 2048, 128], P('grp', 'seq')
Inputs may be any that keep to these rules, and one draw needn't show every extreme that they name: `delta_codes`: for every sequence, head and channel, the running sum of the codes from the sequence's first token lies in -32 .. 31 after every token, and in -2 .. 1 after the last token of each group of 16 tokens.
All inputs are finite; a program needn't handle non-finite values.
Results may differ from a plain program's by a relative error of at most 0.001.
Values may be sent and summed in bfloat16 or wider, within the bound.
A program may use at most 128 MiB of HBM per device.

v0:
```python
import jax
import jax.numpy as jnp
from jax import lax
from jax.sharding import PartitionSpec as P


def lookup_scales(scale_ids, scale_table):
    levels = scale_table.shape[0]
    onehot = (scale_ids[..., None] == jnp.arange(levels, dtype=jnp.int32)).astype(jnp.float32)
    flat = jnp.dot(
        onehot.reshape(-1, levels),
        scale_table,
        precision=lax.Precision.HIGHEST,
        preferred_element_type=jnp.float32,
    )
    return flat.reshape(scale_ids.shape + (scale_table.shape[1],))


def dequantize(code_vals, scale_ids, scale_table):
    head_dim = code_vals.shape[-1]
    steps_len = code_vals.shape[-2]
    groups = scale_ids.shape[-1]
    scales = lookup_scales(scale_ids, scale_table)
    lead_dims = code_vals.shape[:-2]
    shaped = code_vals.astype(jnp.float32).reshape(
        lead_dims + (groups, steps_len // groups, head_dim)
    )
    return (shaped * scales[..., :, None, :]).reshape(code_vals.shape)


def block_prefix(deltas):
    tok_len = deltas.shape[1]
    lower_ones = (jnp.arange(tok_len)[:, None] >= jnp.arange(tok_len)[None, :]).astype(jnp.float32)
    return jnp.einsum("tu,ruc->rtc", lower_ones, deltas, precision=lax.Precision.HIGHEST)


def on_device(delta_codes, scale_index, anchor_codes, scale_table, anchor_scale):
    seq_count = lax.axis_size("seq")
    seq_local, kv_heads, tok_dev, head_dim = delta_codes.shape
    deltas = dequantize(delta_codes, scale_index, scale_table)
    prefix = block_prefix(deltas.reshape(-1, tok_dev, head_dim)).reshape(deltas.shape)
    block_total = prefix[:, :, -1, :]
    anchor_vals = anchor_codes.astype(jnp.float32) * anchor_scale
    every_total = lax.all_gather(block_total[None], "seq", axis=0, tiled=True)
    my_index = lax.axis_index("seq")
    earlier = (jnp.arange(seq_count, dtype=jnp.int32) < my_index).astype(jnp.float32)
    carried = jnp.sum(earlier[:, None, None, None] * every_total, axis=0)
    rebuilt = (prefix + (carried + anchor_vals)[:, :, None, :]).astype(jnp.bfloat16)
    sectioned = lax.all_to_all(rebuilt, "grp", split_axis=1, concat_axis=0, tiled=True)
    result = lax.all_to_all(
        sectioned.reshape(-1, tok_dev, head_dim), "seq", split_axis=0, concat_axis=1, tiled=True
    )
    return result[None]


def solution(mesh):
    placed = (P("grp", None, "seq", None), P("grp", None, "seq"), P("grp", None, None), P(), P())
    return jax.shard_map(
        on_device,
        mesh=mesh,
        in_specs=placed,
        out_specs=P("grp", "seq", None, None),
        check_vma=False,
    )
```

profile of v0, /device:TPU:7, one launch (start us, length us, event | category | flops | bytes accessed | tf_op | source)
XLA Modules:
  0.0 230.9 jit_solution(16256442667135979080)
XLA Ops:
  0.0 0.0 copy-start
  0.0 0.7 copy-done
  0.7 1.2 fusion
  1.9 3.9 %mul.27 = f32[4,16,16,16,128]{4,3,2,1,0:T(8,128)} broadcast(f32[4,16,16,128]{3,2,1,0:T(8,128)S(1)} %fusion), dimensions={0,1,2,4} | broadcast | bytes 8912896 | tf_op jit(solution)/shard_map/mul | solution.py:28
  5.8 11.4 %bitcast_multiply_fusion = f32[64,256,128]{2,1,0:T(8,128)} fusion(f32[64,256,128]{2,1,0:T(8,128)} %bitcast.26, s32[4,16,256,128]{3,2,1,0:T(8,128)} %param.5), kind=kLoop, calls=%fused_computation | loop fusion | flops 4194304 | bytes 25165824 | tf_op jit(solution)/shard_map/mul | solution.py:28
  17.2 9.4 %fusion.3 = f32[64,128,256]{2,1,0:T(8,128)S(1)} fusion(f32[64,256,128]{2,1,0:T(8,128)} %bitcast_multiply_fusion), kind=kOutput, calls=%fused_computation.8 | convolution fusion | flops 6442516480 | bytes 16777216 | tf_op jit(solution)/shard_map/tu,ruc->rtc/dot_general | solution.py:34
  26.6 0.0 copy-start.2
  26.6 3.2 %copy-done.2 = f32[64,128,256]{2,1,0:T(8,128)} copy-done((f32[64,128,256]{2,1,0:T(8,128)}, f32[64,128,256]{2,1,0:T(8,128)S(1)}, u32[]{:S(2)}) %copy-start.2) | copy-done | bytes 8388632
  29.8 3.2 %slice.4 = f32[4,16,1,128]{2,3,1,0:T(8,128)} slice(f32[4,16,256,128]{2,3,1,0:T(8,128)S(1)} %bitcast.24), slice={[0:4], [0:16], [255:256], [0:128]} | slice | bytes 65536 | tf_op jit(solution)/shard_map/slice | solution.py:42
  33.0 0.0 copy-start.3
  33.0 0.0 copy-start.4
  33.0 9.3 %copy.18 = f32[4,16,256,128]{3,2,0,1:T(8,128)} copy(f32[4,16,256,128]{2,3,1,0:T(8,128)} %bitcast.25) | data formatting | bytes 16777216 | tf_op jit(solution)/shard_map/reshape | solution.py:41
  42.3 2.8 %copy.25 = f32[4,16,1,128]{3,1,2,0:T(8,128)S(1)} copy(f32[4,16,1,128]{2,3,1,0:T(8,128)} %slice.4) | data formatting | bytes 65536
  45.1 24.9 %all-gather = f32[32,16,1,128]{3,1,2,0:T(8,128)S(1)} all-gather(f32[4,16,1,128]{3,1,2,0:T(8,128)S(1)} %copy.25), channel_id=2, replica_groups=mesh['seq'=8,'grp'=4] {'seq'}, dimensions={0}, use_global_device_ids=true | all-gather | bytes 294912 | tf_op jit(solution)/shard_map/all_gather | solution.py:44
  69.9 0.1 multiply_reduce_fusion
  70.0 0.0 copy-done.3
  70.0 0.0 copy-done.4
  70.1 4.7 %add_convert_fusion = bf16[4,16,256,128]{3,2,0,1:T(8,128)(2,1)S(1)} fusion(f32[4,16,256,128]{3,2,0,1:T(8,128)} %copy.18, f32[4,16,128]{2,0,1:T(4,128)S(1)} %copy.17), kind=kLoop, calls=%fused_computation.1 | loop fusion | flops 4194304 | bytes 12615680 | tf_op jit(solution)/shard_map/convert_element_type | solution.py:48
  74.8 56.0 %all_to_all.30 = bf16[4,16,256,128]{3,2,0,1:T(8,128)(2,1)S(1)} all-to-all(bf16[4,16,256,128]{3,2,0,1:T(8,128)(2,1)S(1)} %add_convert_fusion), channel_id=1, replica_groups=mesh['seq'=8,'grp'=4] {'grp'}, dimensions={1} | all-to-all | bytes 8388608 | tf_op jit(solution)/shard_map/all_to_all | solution.py:49
  130.8 0.5 copy.20
  131.3 0.0 copy-start.1
  131.3 97.3 %all_to_all.31 = bf16[64,256,128]{2,1,0:T(8,128)(2,1)S(1)} all-to-all(bf16[64,256,128]{2,1,0:T(8,128)(2,1)S(1)} %bitcast.28), channel_id=1, replica_groups=mesh['seq'=8,'grp'=4] {'seq'}, dimensions={0} | all-to-all | bytes 8388608 | tf_op jit(solution)/shard_map/all_to_all | solution.py:50
  228.6 2.3 copy.21
  230.9 0.0 copy-done.1
  (3 shorter events, 0.0 us)
Async XLA Ops:
  0.0 0.7 copy-start
  26.6 3.2 %copy-start.2 = (f32[64,128,256]{2,1,0:T(8,128)}, f32[64,128,256]{2,1,0:T(8,128)S(1)}, u32[]{:S(2)}) copy-start(f32[64,128,256]{2,1,0:T(8,128)S(1)} %fusion.3) | copy-start | bytes 25165828
  33.0 37.0 %copy-start.3 = (s32[4,16,128]{2,1,0:T(8,128)S(1)}, s32[4,16,128]{2,1,0:T(8,128)}, u32[]{:S(2)}) copy-start(s32[4,16,128]{2,1,0:T(8,128)} %param.7) | copy-start | bytes 98308
  33.0 37.1 %copy-start.4 = (f32[128]{0:T(128)S(1)}, f32[128]{0:T(128)}, u32[]{:S(2)}) copy-start(f32[128]{0:T(128)} %param.9) | copy-start | bytes 1540
  131.3 99.7 %copy-start.1 = (f32[16,128]{1,0:T(8,128)S(1)}, f32[16,128]{1,0:T(8,128)}, u32[]{:S(2)}) copy-start(f32[16,128]{1,0:T(8,128)} %param.8) | copy-start | bytes 24580
where the time goes:
time: 235 us; the launch traced here: 231 us
  blocking collectives  178 us (76%)
  local copies, waits for them, and re-layouts  25.9 us (11%)
  other arithmetic  16.2 us (7%)
  matrix products  10.6 us (5%)
    all_to_all x1, blocking collectives, on_device(): lax.all_to_all(sectioned.reshape(-1, tok_dev, head_dim), 'seq', split_axi...  97.3 us
    all_to_all x1, blocking collectives, on_device(): lax.all_to_all(rebuilt, 'grp', split_axis=1, concat_axis=0, tiled=True)  56 us
    all_gather x1, blocking collectives, on_device(): every_total = lax.all_gather(block_total[None], 'seq', axis=0, tiled=True)  24.9 us
    mul x1, other arithmetic, dequantize(): return (shaped * scales[..., :, None, :]).reshape(code_vals.shape)  11.4 us
    dot_general x1, matrix products, block_prefix(): jnp.einsum('tu,ruc->rtc', lower_ones, deltas, precision=lax.Precision.HIG...  9.38 us
    reshape x1, local copies, waits for them, and re-layouts, on_device(): block_prefix(deltas.reshape(-1, tok_dev, head_dim)).reshape(deltas.shape)  9.26 us
    unnamed x11, local copies, waits for them, and re-layouts  6.76 us

commit v1 on v0

v1 whole, which is shorter than its diff:
```python
import functools

import jax
import jax.numpy as jnp
from jax import lax
from jax.experimental import pallas as pl
from jax.experimental.pallas import tpu as pltpu
from jax.sharding import PartitionSpec as P

MESH = pl.DeviceIdType.MESH
HIGHEST = lax.Precision.HIGHEST


def exchange(
    codes, index_ref, anchor_ref, table_ref, anchor_scale_ref,
    landed, scales_ref, base_ref,
    raw, sums, index_out, index_in, anchor_out, anchor_in,
    load_sem, send_sem, recv_sem, isend_sem, irecv_sem, asend_sem, arecv_sem,
):
    seqs, grps = lax.axis_size("seq"), lax.axis_size("grp")
    s, g = lax.axis_index("seq"), lax.axis_index("grp")
    blocks, rows, tokens, channels = sums.shape
    heads = codes.shape[1] // grps
    per_grp = blocks // grps
    seq_rows, head_rows = max(1, rows // heads), min(rows, heads)
    levels = table_ref.shape[0]
    groups = index_ref.shape[2]
    group_len = tokens // groups

    def place(d):
        h = lax.rem(g + d // per_grp, grps)
        i = lax.rem(s + d, per_grp)
        first = i * rows
        return h, g * per_grp + i, first // heads, h * heads + lax.rem(first, heads)

    def is_me(d):
        h, to_s, _, _ = place(d)
        return jnp.logical_and(h == g, to_s == s)

    def load(d):
        _, _, b0, k0 = place(d)
        return pltpu.make_async_copy(
            codes.at[pl.ds(b0, seq_rows), pl.ds(k0, head_rows)], raw.at[d], load_sem.at[d]
        )

    def remote(src, dst, ssem, rsem, d):
        h, to_s, _, _ = place(d)
        return pltpu.make_async_remote_copy(
            src_ref=src, dst_ref=dst, send_sem=ssem, recv_sem=rsem,
            device_id={"seq": to_s, "grp": h}, device_id_type=MESH,
        )

    def window(j):
        return landed.at[:, pl.ds(pl.multiple_of(j * tokens, tokens), tokens), :]

    def send_sums(d):
        return remote(sums.at[d], window(s), send_sem.at[d], recv_sem.at[s], d)

    def send_index(d):
        return remote(index_out.at[d], index_in.at[s], isend_sem.at[d], irecv_sem.at[s], d)

    def send_anchor(d):
        return remote(anchor_out.at[d], anchor_in, asend_sem.at[d], arecv_sem, d)

    @pl.loop(0, blocks)
    def _(d):
        load(d).start()

    barrier = pltpu.get_barrier_semaphore()
    from_g = s // per_grp

    @pl.loop(0, seqs)
    def _(j):
        @pl.when(jnp.logical_not(jnp.logical_and(j == s, from_g == g)))
        def _():
            pl.semaphore_signal(
                barrier, inc=1, device_id={"seq": j, "grp": from_g}, device_id_type=MESH
            )

    kept = jnp.where(from_g == g, 1, 0)

    for d in range(blocks):
        _, _, b0, k0 = place(d)
        for b in range(seq_rows):
            part = pl.ds(b * head_rows, head_rows)
            index_out[d, part, :] = index_ref[b0 + b, pl.ds(k0, head_rows), :]
            anchor_out[d, part, :] = anchor_ref[b0 + b, pl.ds(k0, head_rows), :]

    t_out = lax.broadcasted_iota(jnp.int32, (tokens, tokens), 0)
    t_in = lax.broadcasted_iota(jnp.int32, (tokens, tokens), 1)
    same = t_out // group_len == t_in // group_len
    within = jnp.where(jnp.logical_and(same, t_out >= t_in), 1.0, 0.0).astype(jnp.bfloat16)

    @pl.loop(0, blocks)
    def _(d):
        load(d).wait()
        for r in range(rows):
            x = raw[d, r // head_rows, r % head_rows].astype(jnp.float32).astype(jnp.bfloat16)
            run = jnp.dot(within, x, preferred_element_type=jnp.float32)
            sums[d, r] = run.astype(jnp.bfloat16)

        @pl.when(d == 0)
        def _():
            pl.semaphore_wait(barrier, blocks - kept)

        @pl.when(jnp.logical_not(is_me(d)))
        def _():
            send_index(d).start()

            @pl.when(s == 0)
            def _():
                send_anchor(d).start()

            send_sums(d).start()

    @pl.loop(0, blocks)
    def _(d):
        @pl.when(is_me(d))
        def _():
            index_in[s] = index_out[d]
            for r in range(rows):
                landed[r, pl.ds(pl.multiple_of(s * tokens, tokens), tokens), :] = sums[d, r]

            @pl.when(s == 0)
            def _():
                anchor_in[...] = anchor_out[d]

    mine = jnp.logical_and(from_g == g, s == 0)

    @pl.when(jnp.logical_not(mine))
    def _():
        send_anchor(0).wait_recv()

    for r in range(rows):
        base_ref[r] = anchor_in[pl.ds(r, 1), :].astype(jnp.float32) * anchor_scale_ref[...]

    def from_me(j):
        return jnp.logical_and(j == s, from_g == g)

    @pl.loop(0, seqs)
    def _(j):
        @pl.when(jnp.logical_not(from_me(j)))
        def _():
            remote(index_out.at[0], index_in.at[j], isend_sem.at[0], irecv_sem.at[j], 0).wait_recv()

        table = table_ref[...]
        for r in range(rows):
            ids = jnp.broadcast_to(index_in[j, pl.ds(r, 1), :], (levels, groups))
            hot = (ids == lax.broadcasted_iota(jnp.int32, (levels, groups), 0)).astype(jnp.float32)
            found = lax.dot_general(
                hot, table, (((0,), (0,)), ((), ())),
                precision=HIGHEST, preferred_element_type=jnp.float32,
            )
            scales_ref[r, pl.ds(pl.multiple_of(j * groups, groups), groups), :] = found

    @pl.loop(0, seqs)
    def _(j):
        @pl.when(jnp.logical_not(from_me(j)))
        def _():
            remote(sums.at[0], window(j), send_sem.at[0], recv_sem.at[j], 0).wait_recv()

    @pl.loop(0, blocks)
    def _(d):
        @pl.when(jnp.logical_not(is_me(d)))
        def _():
            send_index(d).wait_send()

            @pl.when(s == 0)
            def _():
                send_anchor(d).wait_send()

            send_sums(d).wait_send()


def rebuild(sums_ref, scales_ref, base_ref, out_ref, carry):
    r, c = pl.program_id(0), pl.program_id(1)
    step, channels = out_ref.shape[2:]
    group_len = sums_ref.shape[1] // scales_ref.shape[1]
    groups = step // group_len

    @pl.when(c == 0)
    def _():
        carry[...] = base_ref[r]

    x = sums_ref[r, pl.ds(pl.multiple_of(c * step, step), step), :]
    x = x.astype(jnp.float32).reshape(groups, group_len, channels)
    scale = scales_ref[r, pl.ds(pl.multiple_of(c * groups, groups), groups), :]
    total = x[:, group_len - 1, :] * scale
    row = lax.broadcasted_iota(jnp.int32, (groups, groups), 0)
    col = lax.broadcasted_iota(jnp.int32, (groups, groups), 1)
    earlier = (row > col).astype(jnp.float32)
    base = jnp.dot(
        earlier, total, precision=HIGHEST, preferred_element_type=jnp.float32
    ) + carry[...]
    carry[...] = base[groups - 1:] + total[groups - 1:]
    out = x * scale[:, None, :] + base[:, None, :]
    out_ref[0, 0] = out.reshape(groups * group_len, channels).astype(jnp.bfloat16)


def on_device(delta_codes, scale_index, anchor_codes, scale_table, anchor_scale):
    seqs, grps = lax.axis_size("seq"), lax.axis_size("grp")
    seq_local, kv_heads, tokens, channels = delta_codes.shape
    groups = scale_index.shape[2]
    heads = kv_heads // grps
    rows = seq_local * grps * heads // seqs
    blocks = seq_local * kv_heads // rows
    seq_rows, head_rows = max(1, rows // heads), min(rows, heads)
    length = seqs * tokens
    vmem = pl.BlockSpec(memory_space=pltpu.VMEM)
    hbm = pl.BlockSpec(memory_space=pltpu.HBM)
    sums, scales, base = pl.pallas_call(
        exchange,
        out_shape=(
            jax.ShapeDtypeStruct((rows, length, channels), jnp.bfloat16),
            jax.ShapeDtypeStruct((rows, seqs * groups, channels), jnp.float32),
            jax.ShapeDtypeStruct((rows, 1, channels), jnp.float32),
        ),
        in_specs=[hbm, vmem, vmem, vmem, vmem],
        out_specs=(vmem, vmem, vmem),
        scratch_shapes=[
            pltpu.VMEM((blocks, seq_rows, head_rows, tokens, channels), jnp.int32),
            pltpu.VMEM((blocks, rows, tokens, channels), jnp.bfloat16),
            pltpu.VMEM((blocks, rows, groups), jnp.int32),
            pltpu.VMEM((seqs, rows, groups), jnp.int32),
            pltpu.VMEM((blocks, rows, channels), jnp.int32),
            pltpu.VMEM((rows, channels), jnp.int32),
            pltpu.SemaphoreType.DMA((blocks,)),
            pltpu.SemaphoreType.DMA((blocks,)),
            pltpu.SemaphoreType.DMA((seqs,)),
            pltpu.SemaphoreType.DMA((blocks,)),
            pltpu.SemaphoreType.DMA((seqs,)),
            pltpu.SemaphoreType.DMA((blocks,)),
            pltpu.SemaphoreType.DMA,
        ],
        compiler_params=pltpu.CompilerParams(
            collective_id=0, has_side_effects=True, vmem_limit_bytes=56 * 1024 * 1024
        ),
        name="exchange",
    )(delta_codes, scale_index, anchor_codes, scale_table, anchor_scale[None])

    step = 4 * tokens
    out = pl.pallas_call(
        rebuild,
        grid=(rows, length // step),
        out_shape=jax.ShapeDtypeStruct((1, rows, length, channels), jnp.bfloat16),
        in_specs=[vmem, vmem, vmem],
        out_specs=pl.BlockSpec((1, 1, step, channels), lambda r, c: (0, r, c, 0)),
        scratch_shapes=[pltpu.VMEM((1, channels), jnp.float32)],
        compiler_params=pltpu.CompilerParams(vmem_limit_bytes=16 * 1024 * 1024),
        name="rebuild",
    )(sums, scales, base)
    return out


def solution(mesh):
    placed = (P("grp", None, "seq", None), P("grp", None, "seq"), P("grp", None, None), P(), P())
    return jax.shard_map(
        on_device,
        mesh=mesh,
        in_specs=placed,
        out_specs=P("grp", "seq", None, None),
        check_vma=False,
    )
```

time: 235 us -> 202 us (0.86); the launches traced: 231 us -> 202 us
  Pallas kernels: 0 us -> 198 us
  blocking collectives: 178 us -> 0 us
  local copies, waits for them, and re-layouts: 25.9 us -> 3.9 us
  other arithmetic: 16.2 us -> 0 us
  matrix products: 10.6 us -> 0 us
    pallas_call x0 -> x2, Pallas kernels: none -> 198 us  [the longest x1 190 us: on_device(): pl.pallas_call(exchange, out_shape=(jax.ShapeDtypeStruct((rows, length, c...]
    all_to_all x2 -> x0, blocking collectives: 153 us -> none  [the longest x1 97.3 us: on_device(): lax.all_to_all(sectioned.reshape(-1, tok_dev, head_dim), 'seq', split_axi...]
    all_gather x1 -> x0, blocking collectives: 24.9 us -> none  [on_device(): every_total = lax.all_gather(block_total[None], 'seq', axis=0, tiled=True)]
    mul x1 -> x0, other arithmetic: 11.4 us -> none  [dequantize(): return (shaped * scales[..., :, None, :]).reshape(code_vals.shape)]
    dot_general x2 -> x0, matrix products: 10.6 us -> none  [the longest x1 9.38 us: block_prefix(): jnp.einsum('tu,ruc->rtc', lower_ones, deltas, precision=lax.Precision.HIG...]
    reshape x1 -> x0, local copies, waits for them, and re-layouts: 9.26 us -> none  [on_device(): block_prefix(deltas.reshape(-1, tok_dev, head_dim)).reshape(deltas.shape)]
    convert_element_type x2 -> x0, other arithmetic: 4.7 us -> none  [the longest x1 4.69 us: on_device(): (prefix + (carried + anchor_vals)[:, :, None, :]).astype(jnp.bfloat16)]
    mul x1 -> x0, local copies, waits for them, and re-layouts: 3.91 us -> none  [dequantize(): return (shaped * scales[..., :, None, :]).reshape(code_vals.shape)]
where the time goes in v1:
time: 202 us
  Pallas kernels  198 us (98%)
  local copies, waits for them, and re-layouts  3.9 us (2%)
    pallas_call x1, Pallas kernels, on_device(): pl.pallas_call(exchange, out_shape=(jax.ShapeDtypeStruct((rows, length, c...  190 us
    pallas_call x1, Pallas kernels, on_device(): pl.pallas_call(rebuild, grid=(rows, length // step), out_shape=jax.ShapeD...  7.75 us

profile of v1, /device:TPU:7, one launch (start us, length us, event | category | flops | bytes accessed | tf_op | source)
XLA Modules:
  0.0 202.0 jit_solution(11260204702739048905)
XLA Ops:
  0.0 190.4 %exchange.1 = (bf16[8,2048,128]{2,1,0:T(8,128)(2,1)}, f32[8,128,128]{2,1,0:T(8,128)}, f32[8,1,128]{2,1,0:T(1,128)}) custom-call(s32[4,16,256,128]{3,2,1,0:T(8,128)} %codes.1, s32[4,16,16]{2,1,0:T(8,128)} %index_ref.1, s32[4,16,128]{2,1,0:T(8,128)} %anchor_ref.1, f32[16,128]{1,0:T(8,128)} %table_ref.1, f32[1,128]{1,0:T(1,128)} %bitcast.1), custom_call_target="tpu_custom_call" | custom-call | tf_op jit(solution)/shard_map/exchange/pallas_call | solution.py:211
  190.4 0.0 copy-start
  190.4 2.2 %copy-done = bf16[8,2048,128]{2,1,0:T(8,128)(2,1)S(1)} copy-done((bf16[8,2048,128]{2,1,0:T(8,128)(2,1)S(1)}, bf16[8,2048,128]{2,1,0:T(8,128)(2,1)}, u32[]{:S(2)}) %copy-start) | copy-done | bytes 4194328
  192.6 0.0 copy-start.1
  192.6 1.0 copy-done.1
  193.6 0.0 copy-start.2
  193.6 0.7 copy-done.2
  194.3 7.8 %rebuild.1 = bf16[1,8,2048,128]{3,2,1,0:T(8,128)(2,1)} custom-call(bf16[8,2048,128]{2,1,0:T(8,128)(2,1)S(1)} %copy-done, f32[8,128,128]{2,1,0:T(8,128)S(1)} %copy-done.1, f32[8,1,128]{2,1,0:T(1,128)S(1)} %copy-done.2), custom_call_target="tpu_custom_call" | custom-call | tf_op jit(solution)/shard_map/rebuild/pallas_call | solution.py:242
Async XLA Ops:
  190.4 2.2 %copy-start = (bf16[8,2048,128]{2,1,0:T(8,128)(2,1)S(1)}, bf16[8,2048,128]{2,1,0:T(8,128)(2,1)}, u32[]{:S(2)}) copy-start(bf16[8,2048,128]{2,1,0:T(8,128)(2,1)} %get-tuple-element.8.sums_ref) | copy-start | bytes 12582916
  192.6 1.0 copy-start.1
  193.6 0.7 copy-start.2

commit v2 on v1

--- a/solution.py
+++ b/solution.py
@@ -8,30 +8,42 @@
 from jax.sharding import PartitionSpec as P
 
 MESH = pl.DeviceIdType.MESH
+CHUNKS = 4
 HIGHEST = lax.Precision.HIGHEST
 
 
 def exchange(
     codes, index_ref, anchor_ref, table_ref, anchor_scale_ref,
     landed, scales_ref, base_ref,
-    raw, sums, index_out, index_in, anchor_out, anchor_in,
+    raw, sums, relay, index_out, index_in, anchor_out, anchor_in,
     load_sem, send_sem, recv_sem, isend_sem, irecv_sem, asend_sem, arecv_sem,
+    relay_sem, forward_sem,
 ):
     seqs, grps = lax.axis_size("seq"), lax.axis_size("grp")
     s, g = lax.axis_index("seq"), lax.axis_index("grp")
     blocks, rows, tokens, channels = sums.shape
     heads = codes.shape[1] // grps
     per_grp = blocks // grps
+    half = grps // 2
+    partner = lax.rem(g + half, grps)
+    chunks = relay.shape[1]
+    chunk_rows = rows // chunks
+    passed = blocks // 2 * chunks
     seq_rows, head_rows = max(1, rows // heads), min(rows, heads)
     levels = table_ref.shape[0]
     groups = index_ref.shape[2]
     group_len = tokens // groups
 
+    def place_from(d, own):
+        e = d // 2
+        side = lax.rem(own // half + 1 + d, 2)
+        h = side * half + lax.rem(own + e // per_grp, half)
+        i = lax.rem(s + e, per_grp)
+        first = i * rows
+        return h, own * per_grp + i, first // heads, h * heads + lax.rem(first, heads)
+
     def place(d):
-        h = lax.rem(g + d // per_grp, grps)
-        i = lax.rem(s + d, per_grp)
-        first = i * rows
-        return h, g * per_grp + i, first // heads, h * heads + lax.rem(first, heads)
+        return place_from(d, g)
 
     def is_me(d):
         h, to_s, _, _ = place(d)
@@ -56,6 +68,38 @@
     def send_sums(d):
         return remote(sums.at[d], window(s), send_sem.at[d], recv_sem.at[s], d)
 
+    def at_partner(d):
+        h, to_s, _, _ = place(d)
+        return jnp.logical_and(h == partner, to_s == s)
+
+    def send_relay(e, c):
+        return pltpu.make_async_remote_copy(
+            src_ref=sums.at[2 * e, pl.ds(c * chunk_rows, chunk_rows)], dst_ref=relay.at[e, c],
+            send_sem=send_sem.at[2 * e], recv_sem=relay_sem.at[e, c],
+            device_id={"seq": s, "grp": partner}, device_id_type=MESH,
+        )
+
+    def relayed(e):
+        h, to_s, _, _ = place_from(2 * e, partner)
+        return jnp.logical_not(jnp.logical_and(h == g, to_s == s))
+
+    def forward(e, c):
+        h, to_s, _, _ = place_from(2 * e, partner)
+        span = pl.ds(pl.multiple_of(s * tokens, tokens), tokens)
+        return pltpu.make_async_remote_copy(
+            src_ref=relay.at[e, c], dst_ref=landed.at[pl.ds(c * chunk_rows, chunk_rows), span, :],
+            send_sem=forward_sem.at[e], recv_sem=recv_sem.at[s],
+            device_id={"seq": to_s, "grp": h}, device_id_type=MESH,
+        )
+
+    def pass_on(n):
+        e, c = n // chunks, lax.rem(n, chunks)
+
+        @pl.when(relayed(e))
+        def _():
+            send_relay(e, c).wait_recv()
+            forward(e, c).start()
+
     def send_index(d):
         return remote(index_out.at[d], index_in.at[s], isend_sem.at[d], irecv_sem.at[s], d)
 
@@ -69,15 +113,26 @@
     barrier = pltpu.get_barrier_semaphore()
     from_g = s // per_grp
 
-    @pl.loop(0, seqs)
-    def _(j):
-        @pl.when(jnp.logical_not(jnp.logical_and(j == s, from_g == g)))
+    inside = lax.rem(from_g, half) == lax.rem(g, half)
+
+    @pl.loop(0, 2 * seqs)
+    def _(n):
+        j = n // 2
+        to_g = lax.rem(from_g + lax.rem(n, 2) * half, grps)
+
+        @pl.when(jnp.logical_not(jnp.logical_and(j == s, to_g == g)))
         def _():
             pl.semaphore_signal(
-                barrier, inc=1, device_id={"seq": j, "grp": from_g}, device_id_type=MESH
+                barrier, inc=1, device_id={"seq": j, "grp": to_g}, device_id_type=MESH
             )
 
-    kept = jnp.where(from_g == g, 1, 0)
+    @pl.when(jnp.logical_not(inside))
+    def _():
+        pl.semaphore_signal(
+            barrier, inc=1, device_id={"seq": s, "grp": partner}, device_id_type=MESH
+        )
+
+    expected = 2 * blocks + jnp.where(inside, -1, 1)
 
     for d in range(blocks):
         _, _, b0, k0 = place(d)
@@ -101,7 +156,7 @@
 
         @pl.when(d == 0)
         def _():
-            pl.semaphore_wait(barrier, blocks - kept)
+            pl.semaphore_wait(barrier, expected)
 
         @pl.when(jnp.logical_not(is_me(d)))
         def _():
@@ -111,7 +166,24 @@
             def _():
                 send_anchor(d).start()
 
-            send_sums(d).start()
+            via = jnp.logical_and(lax.rem(d, 2) == 0, jnp.logical_not(at_partner(d)))
+
+            @pl.when(via)
+            def _():
+                for c in range(chunks):
+                    send_relay(d // 2, c).start()
+
+            @pl.when(jnp.logical_not(via))
+            def _():
+                send_sums(d).start()
+
+        @pl.when(jnp.logical_and(d >= 2, d - 2 < passed))
+        def _():
+            pass_on(d - 2)
+
+    @pl.loop(min(blocks - 2, passed), passed)
+    def _(n):
+        pass_on(n)
 
     @pl.loop(0, blocks)
     def _(d):
@@ -170,6 +242,13 @@
                 send_anchor(d).wait_send()
 
             send_sums(d).wait_send()
+
+    @pl.loop(0, blocks // 2)
+    def _(e):
+        @pl.when(relayed(e))
+        def _():
+            for c in range(chunks):
+                forward(e, c).wait_send()
 
 
 def rebuild(sums_ref, scales_ref, base_ref, out_ref, carry):
@@ -205,6 +284,7 @@
     rows = seq_local * grps * heads // seqs
     blocks = seq_local * kv_heads // rows
     seq_rows, head_rows = max(1, rows // heads), min(rows, heads)
+    chunks = min(rows, CHUNKS)
     length = seqs * tokens
     vmem = pl.BlockSpec(memory_space=pltpu.VMEM)
     hbm = pl.BlockSpec(memory_space=pltpu.HBM)
@@ -220,6 +300,7 @@
         scratch_shapes=[
             pltpu.VMEM((blocks, seq_rows, head_rows, tokens, channels), jnp.int32),
             pltpu.VMEM((blocks, rows, tokens, channels), jnp.bfloat16),
+            pltpu.VMEM((blocks // 2, chunks, rows // chunks, tokens, channels), jnp.bfloat16),
             pltpu.VMEM((blocks, rows, groups), jnp.int32),
             pltpu.VMEM((seqs, rows, groups), jnp.int32),
             pltpu.VMEM((blocks, rows, channels), jnp.int32),
@@ -231,9 +312,11 @@
             pltpu.SemaphoreType.DMA((seqs,)),
             pltpu.SemaphoreType.DMA((blocks,)),
             pltpu.SemaphoreType.DMA,
+            pltpu.SemaphoreType.DMA((blocks // 2, chunks)),
+            pltpu.SemaphoreType.DMA((blocks // 2,)),
         ],
         compiler_params=pltpu.CompilerParams(
-            collective_id=0, has_side_effects=True, vmem_limit_bytes=56 * 1024 * 1024
+            collective_id=0, has_side_effects=True, vmem_limit_bytes=48 * 1024 * 1024
         ),
         name="exchange",
     )(delta_codes, scale_index, anchor_codes, scale_table, anchor_scale[None])

time: 202 us -> 113 us (0.56)
  Pallas kernels: 198 us -> 110 us
    pallas_call x1, Pallas kernels: 190 us -> 102 us  [on_device(): pl.pallas_call(exchange, out_shape=(jax.ShapeDtypeStruct((rows, length, c...]
where the time goes in v2:
time: 113 us
  Pallas kernels  110 us (97%)
  local copies, waits for them, and re-layouts  2.87 us (3%)
    pallas_call x1, Pallas kernels, on_device(): pl.pallas_call(exchange, out_shape=(jax.ShapeDtypeStruct((rows, length, c...  102 us
    pallas_call x1, Pallas kernels, on_device(): pl.pallas_call(rebuild, grid=(rows, length // step), out_shape=jax.ShapeD...  7.78 us
    unnamed x8, local copies, waits for them, and re-layouts  2.87 us

profile of v2, /device:TPU:7, one launch (start us, length us, event | category | flops | bytes accessed | tf_op | source)
XLA Modules:
  0.0 112.9 jit_solution(4153249513556158538)
XLA Ops:
  0.0 0.0 copy-start
  0.0 0.8 copy-done
  0.8 0.0 copy-start.1
  0.8 0.8 copy-done.1
  1.5 0.0 copy-start.2
  1.5 0.7 copy-done.2
  2.2 0.0 copy-start.3
  2.2 0.7 copy-done.3
  2.9 102.2 %exchange.1 = (bf16[8,2048,128]{2,1,0:T(8,128)(2,1)S(1)}, f32[8,128,128]{2,1,0:T(8,128)S(1)}, f32[8,1,128]{2,1,0:T(1,128)S(1)}) custom-call(s32[4,16,256,128]{3,2,1,0:T(8,128)} %codes.1, s32[4,16,16]{2,1,0:T(8,128)S(1)} %copy-done, s32[4,16,128]{2,1,0:T(8,128)S(1)} %copy-done.1, f32[16,128]{1,0:T(8,128)S(1)} %copy-done.2, f32[1,128]{1,0:T(1,128)S(1)} %bitcast.1), custom_call_target="tpu_custom_call" | custom-call | tf_op jit(solution)/shard_map/exchange/pallas_call | solution.py:291
  105.1 7.8 %rebuild.1 = bf16[1,8,2048,128]{3,2,1,0:T(8,128)(2,1)} custom-call(bf16[8,2048,128]{2,1,0:T(8,128)(2,1)S(1)} %get-tuple-element.8.sums_ref, f32[8,128,128]{2,1,0:T(8,128)S(1)} %get-tuple-element.9.scales_ref, f32[8,1,128]{2,1,0:T(1,128)S(1)} %get-tuple-element.10.base_ref), custom_call_target="tpu_custom_call" | custom-call | tf_op jit(solution)/shard_map/rebuild/pallas_call | solution.py:325
Async XLA Ops:
  0.0 0.8 copy-start
  0.8 0.8 copy-start.1
  1.5 0.7 copy-start.2
  2.2 0.7 copy-start.3

commit v3 on v2

--- a/solution.py
+++ b/solution.py
@@ -9,15 +9,17 @@
 
 MESH = pl.DeviceIdType.MESH
 CHUNKS = 4
+LAG = 1
 HIGHEST = lax.Precision.HIGHEST
 
 
 def exchange(
-    codes, index_ref, anchor_ref, table_ref, anchor_scale_ref,
+    codes, index_hbm, anchor_hbm, table_hbm, anchor_scale_hbm,
     landed, scales_ref, base_ref,
     raw, sums, relay, index_out, index_in, anchor_out, anchor_in,
     load_sem, send_sem, recv_sem, isend_sem, irecv_sem, asend_sem, arecv_sem,
     relay_sem, forward_sem,
+    index_ref, anchor_ref, table_ref, anchor_scale_ref, small_sem,
 ):
     seqs, grps = lax.axis_size("seq"), lax.axis_size("grp")
     s, g = lax.axis_index("seq"), lax.axis_index("grp")
@@ -31,7 +33,7 @@
     passed = blocks // 2 * chunks
     seq_rows, head_rows = max(1, rows // heads), min(rows, heads)
     levels = table_ref.shape[0]
-    groups = index_ref.shape[2]
+    groups = index_hbm.shape[2]
     group_len = tokens // groups
 
     def place_from(d, own):
@@ -72,11 +74,20 @@
         h, to_s, _, _ = place(d)
         return jnp.logical_and(h == partner, to_s == s)
 
+    def part(c):
+        return pl.ds(c * chunk_rows, chunk_rows)
+
     def send_relay(e, c):
         return pltpu.make_async_remote_copy(
-            src_ref=sums.at[2 * e, pl.ds(c * chunk_rows, chunk_rows)], dst_ref=relay.at[e, c],
+            src_ref=sums.at[2 * e, part(c)], dst_ref=relay.at[e, c],
             send_sem=send_sem.at[2 * e], recv_sem=relay_sem.at[e, c],
             device_id={"seq": s, "grp": partner}, device_id_type=MESH,
+        )
+
+    def send_part(d, c):
+        span = pl.ds(pl.multiple_of(s * tokens, tokens), tokens)
+        return remote(
+            sums.at[d, part(c)], landed.at[part(c), span, :], send_sem.at[d], recv_sem.at[s], d
         )
 
     def relayed(e):
@@ -106,9 +117,19 @@
     def send_anchor(d):
         return remote(anchor_out.at[d], anchor_in, asend_sem.at[d], arecv_sem, d)
 
-    @pl.loop(0, blocks)
-    def _(d):
+    ahead = min(2, blocks)
+    for d in range(ahead):
         load(d).start()
+
+    small = (
+        (index_hbm, index_ref), (anchor_hbm, anchor_ref),
+        (table_hbm, table_ref), (anchor_scale_hbm, anchor_scale_ref),
+    )
+    fetches = [
+        pltpu.make_async_copy(src, dst, small_sem.at[n]) for n, (src, dst) in enumerate(small)
+    ]
+    for fetch in fetches:
+        fetch.start()
 
     barrier = pltpu.get_barrier_semaphore()
     from_g = s // per_grp
@@ -134,13 +155,6 @@
 
     expected = 2 * blocks + jnp.where(inside, -1, 1)
 
-    for d in range(blocks):
-        _, _, b0, k0 = place(d)
-        for b in range(seq_rows):
-            part = pl.ds(b * head_rows, head_rows)
-            index_out[d, part, :] = index_ref[b0 + b, pl.ds(k0, head_rows), :]
-            anchor_out[d, part, :] = anchor_ref[b0 + b, pl.ds(k0, head_rows), :]
-
     t_out = lax.broadcasted_iota(jnp.int32, (tokens, tokens), 0)
     t_in = lax.broadcasted_iota(jnp.int32, (tokens, tokens), 1)
     same = t_out // group_len == t_in // group_len
@@ -149,14 +163,47 @@
     @pl.loop(0, blocks)
     def _(d):
         load(d).wait()
-        for r in range(rows):
-            x = raw[d, r // head_rows, r % head_rows].astype(jnp.float32).astype(jnp.bfloat16)
-            run = jnp.dot(within, x, preferred_element_type=jnp.float32)
-            sums[d, r] = run.astype(jnp.bfloat16)
-
-        @pl.when(d == 0)
-        def _():
-            pl.semaphore_wait(barrier, expected)
+
+        @pl.when(d + ahead < blocks)
+        def _():
+            load(d + ahead).start()
+
+        away = jnp.logical_not(is_me(d))
+        via = jnp.logical_and(lax.rem(d, 2) == 0, jnp.logical_not(at_partner(d)))
+        straight = jnp.logical_and(away, jnp.logical_not(via))
+        for c in range(chunks):
+            for r in range(c * chunk_rows, (c + 1) * chunk_rows):
+                x = raw[d, r // head_rows, r % head_rows].astype(jnp.float32).astype(jnp.bfloat16)
+                run = jnp.dot(within, x, preferred_element_type=jnp.float32)
+                sums[d, r] = run.astype(jnp.bfloat16)
+
+            if c == 0:
+                @pl.when(d == 0)
+                def _():
+                    pl.semaphore_wait(barrier, expected)
+
+            @pl.when(via)
+            def _():
+                send_relay(d // 2, c).start()
+
+            @pl.when(straight)
+            def _():
+                send_part(d, c).start()
+
+        @pl.when(jnp.logical_and(d >= LAG, d - LAG < passed))
+        def _():
+            pass_on(d - LAG)
+
+    for fetch in fetches:
+        fetch.wait()
+
+    @pl.loop(0, blocks)
+    def _(d):
+        _, _, b0, k0 = place(d)
+        for b in range(seq_rows):
+            these = pl.ds(b * head_rows, head_rows)
+            index_out[d, these, :] = index_ref[b0 + b, pl.ds(k0, head_rows), :]
+            anchor_out[d, these, :] = anchor_ref[b0 + b, pl.ds(k0, head_rows), :]
 
         @pl.when(jnp.logical_not(is_me(d)))
         def _():
@@ -166,22 +213,7 @@
             def _():
                 send_anchor(d).start()
 
-            via = jnp.logical_and(lax.rem(d, 2) == 0, jnp.logical_not(at_partner(d)))
-
-            @pl.when(via)
-            def _():
-                for c in range(chunks):
-                    send_relay(d // 2, c).start()
-
-            @pl.when(jnp.logical_not(via))
-            def _():
-                send_sums(d).start()
-
-        @pl.when(jnp.logical_and(d >= 2, d - 2 < passed))
-        def _():
-            pass_on(d - 2)
-
-    @pl.loop(min(blocks - 2, passed), passed)
+    @pl.loop(min(blocks - LAG, passed), passed)
     def _(n):
         pass_on(n)
 
@@ -251,29 +283,24 @@
                 forward(e, c).wait_send()
 
 
-def rebuild(sums_ref, scales_ref, base_ref, out_ref, carry):
-    r, c = pl.program_id(0), pl.program_id(1)
-    step, channels = out_ref.shape[2:]
-    group_len = sums_ref.shape[1] // scales_ref.shape[1]
-    groups = step // group_len
-
-    @pl.when(c == 0)
-    def _():
-        carry[...] = base_ref[r]
-
-    x = sums_ref[r, pl.ds(pl.multiple_of(c * step, step), step), :]
-    x = x.astype(jnp.float32).reshape(groups, group_len, channels)
-    scale = scales_ref[r, pl.ds(pl.multiple_of(c * groups, groups), groups), :]
-    total = x[:, group_len - 1, :] * scale
-    row = lax.broadcasted_iota(jnp.int32, (groups, groups), 0)
-    col = lax.broadcasted_iota(jnp.int32, (groups, groups), 1)
-    earlier = (row > col).astype(jnp.float32)
-    base = jnp.dot(
-        earlier, total, precision=HIGHEST, preferred_element_type=jnp.float32
-    ) + carry[...]
-    carry[...] = base[groups - 1:] + total[groups - 1:]
-    out = x * scale[:, None, :] + base[:, None, :]
-    out_ref[0, 0] = out.reshape(groups * group_len, channels).astype(jnp.bfloat16)
+def rebuild(sums_ref, scales_ref, base_ref, out_hbm, built, out_sem):
+    many, length, channels = built.shape
+    groups = scales_ref.shape[1]
+    group_len = length // groups
+    stores = [pltpu.make_async_copy(built.at[r], out_hbm.at[0, r], out_sem.at[r]) for r in range(many)]
+    for r in range(many):
+
+        def step(j, base, r=r):
+            at = pl.multiple_of(j * group_len, group_len)
+            x = sums_ref[r, pl.ds(at, group_len), :].astype(jnp.float32)
+            grown = x * scales_ref[r, pl.ds(j, 1), :]
+            built[r, pl.ds(at, group_len), :] = (grown + base).astype(jnp.bfloat16)
+            return base + grown[group_len - 1:]
+
+        lax.fori_loop(0, groups, step, base_ref[r], unroll=16)
+        stores[r].start()
+    for copy in stores:
+        copy.wait()
 
 
 def on_device(delta_codes, scale_index, anchor_codes, scale_table, anchor_scale):
@@ -295,7 +322,7 @@
             jax.ShapeDtypeStruct((rows, seqs * groups, channels), jnp.float32),
             jax.ShapeDtypeStruct((rows, 1, channels), jnp.float32),
         ),
-        in_specs=[hbm, vmem, vmem, vmem, vmem],
+        in_specs=[hbm] * 5,
         out_specs=(vmem, vmem, vmem),
         scratch_shapes=[
             pltpu.VMEM((blocks, seq_rows, head_rows, tokens, channels), jnp.int32),
@@ -314,6 +341,11 @@
             pltpu.SemaphoreType.DMA,
             pltpu.SemaphoreType.DMA((blocks // 2, chunks)),
             pltpu.SemaphoreType.DMA((blocks // 2,)),
+            pltpu.VMEM(scale_index.shape, jnp.int32),
+            pltpu.VMEM(anchor_codes.shape, jnp.int32),
+            pltpu.VMEM(scale_table.shape, jnp.float32),
+            pltpu.VMEM((1, channels), jnp.float32),
+            pltpu.SemaphoreType.DMA((4,)),
         ],
         compiler_params=pltpu.CompilerParams(
             collective_id=0, has_side_effects=True, vmem_limit_bytes=48 * 1024 * 1024
@@ -321,14 +353,15 @@
         name="exchange",
     )(delta_codes, scale_index, anchor_codes, scale_table, anchor_scale[None])
 
-    step = 4 * tokens
     out = pl.pallas_call(
         rebuild,
-        grid=(rows, length // step),
         out_shape=jax.ShapeDtypeStruct((1, rows, length, channels), jnp.bfloat16),
-        in_specs=[vmem, vmem, vmem],
-        out_specs=pl.BlockSpec((1, 1, step, channels), lambda r, c: (0, r, c, 0)),
-        scratch_shapes=[pltpu.VMEM((1, channels), jnp.float32)],
+        in_specs=[vmem] * 3,
+        out_specs=hbm,
+        scratch_shapes=[
+            pltpu.VMEM(sums.shape, jnp.bfloat16),
+            pltpu.SemaphoreType.DMA((rows,)),
+        ],
         compiler_params=pltpu.CompilerParams(vmem_limit_bytes=16 * 1024 * 1024),
         name="rebuild",
     )(sums, scales, base)

time: 113 us -> 109 us (0.965)
  Pallas kernels: 110 us -> 105 us
    pallas_call x1, Pallas kernels: 7.78 us -> 3.33 us  [on_device(): pl.pallas_call(rebuild, out_shape=jax.ShapeDtypeStruct((1, rows, length,...]
where the time goes in v3:
time: 109 us; the launch traced here: 108 us
  Pallas kernels  105 us (96%)
  local copies, waits for them, and re-layouts  2.87 us (3%)
    pallas_call x1, Pallas kernels, on_device(): pl.pallas_call(exchange, out_shape=(jax.ShapeDtypeStruct((rows, length, c...  102 us
    pallas_call x1, Pallas kernels, on_device(): pl.pallas_call(rebuild, out_shape=jax.ShapeDtypeStruct((1, rows, length,...  3.33 us
    unnamed x8, local copies, waits for them, and re-layouts  2.87 us

profile of v3, /device:TPU:7, one launch (start us, length us, event | category | flops | bytes accessed | tf_op | source)
XLA Modules:
  0.0 108.2 jit_solution(15752198297326599527)
XLA Ops:
  0.0 0.0 copy-start
  0.0 0.8 copy-done
  0.8 0.0 copy-start.1
  0.8 0.8 copy-done.1
  1.5 0.0 copy-start.2
  1.5 0.7 copy-done.2
  2.2 0.0 copy-start.3
  2.2 0.7 copy-done.3
  2.9 102.0 %exchange.1 = (bf16[8,2048,128]{2,1,0:T(8,128)(2,1)S(1)}, f32[8,128,128]{2,1,0:T(8,128)S(1)}, f32[8,1,128]{2,1,0:T(1,128)S(1)}) custom-call(s32[4,16,256,128]{3,2,1,0:T(8,128)} %codes.1, s32[4,16,16]{2,1,0:T(8,128)S(1)} %copy-done, s32[4,16,128]{2,1,0:T(8,128)S(1)} %copy-done.1, f32[16,128]{1,0:T(8,128)S(1)} %copy-done.2, f32[1,128]{1,0:T(1,128)S(1)} %bitcast.1), custom_call_target="tpu_custom_call" | custom-call | tf_op jit(solution)/shard_map/exchange/pallas_call | solution.py:318
  104.9 3.3 %rebuild.1 = bf16[1,8,2048,128]{3,2,1,0:T(8,128)(2,1)} custom-call(bf16[8,2048,128]{2,1,0:T(8,128)(2,1)S(1)} %get-tuple-element.8.sums_ref, f32[8,128,128]{2,1,0:T(8,128)S(1)} %get-tuple-element.9.scales_ref, f32[8,1,128]{2,1,0:T(1,128)S(1)} %get-tuple-element.10.base_ref), custom_call_target="tpu_custom_call" | custom-call | tf_op jit(solution)/shard_map/rebuild/pallas_call | solution.py:356
Async XLA Ops:
  0.0 0.8 copy-start
  0.8 0.8 copy-start.1
  1.5 0.7 copy-start.2
  2.2 0.7 copy-start.3
